TPU v7x, 32 devices: a whole 2x2x4 slice. The times are simulated.
32 devices in a mesh: dom: 16 (over z, y, x), col: 2 (over core).
Axes of the slice: x: 2, y: 2, z: 4, core: 2. Of those that a mesh axis runs over, the one named last changes fastest.
Arguments:
- features: bfloat16 [16384, 256], P(('dom', 'col')), may hold values from -6 to 6
- weight: bfloat16 [256, 256], replicated, may hold values from -0.375 to 0.375
- cotangent: bfloat16 [16384, 256], P(('dom', 'col')), may hold values from -6 to 6
- tile_values: bfloat16 [1280, 128, 128], P(('dom', 'col')), may hold values from -0.15625 to 0.15625
- tile_rows: int32 [1280], P(('dom', 'col')), may hold values from 0 to 7
- tile_cols: int32 [1280], P(('dom', 'col')), may hold values from 0 to 19, as said below
- tile_count: int32 [32], P(('dom', 'col')), may hold values from 20 to 40, as said below
- send_blocks: int32 [32, 16], P(('dom', 'col')), may hold values from 0 to 3
Outputs:
- output_rows: bfloat16 [16384, 256], P(('dom', 'col'))
- feature_grad: bfloat16 [16384, 256], P(('dom', 'col'))
- weight_grad: float32 [256, 256], replicated
Inputs may be any that keep to these rules, and one draw needn't show every extreme that they name: `tile_cols`: A value v below 4 names the device's own row block v; a value 4 + s names the row block that the device of partition s with the same col index sends to this partition; no receive slot is named by two tiles of one device. Only the first tile_count slots of a device's tiles are live; some device has all 40 live.
All inputs are finite; a program needn't handle non-finite values.
Results may differ from a plain program's by a relative error of at most 0.0049.
Values may be sent and summed in bfloat16 or wider, within the bound.
A program may use at most 128 MiB of HBM per device.

v0:
```python
import jax
import jax.numpy as jnp
from jax import lax
from jax.sharding import PartitionSpec as P


def local(features, weight, cotangent, tile_values, tile_rows, tile_cols, tile_count, send_blocks):
    block_size = tile_values.shape[1]
    half_blocks = features.shape[0] // block_size
    width_in = features.shape[1]
    peer_count = send_blocks.shape[1]
    all_blocks = half_blocks * lax.axis_size("col")
    node_total = features.shape[0] * lax.axis_size("col") * lax.axis_size("dom")
    own_blocks = features.reshape(half_blocks, block_size, width_in)
    outgoing = own_blocks[send_blocks[0]]
    incoming = lax.all_to_all(outgoing, "dom", split_axis=0, concat_axis=0, tiled=True)
    sources = jnp.concatenate([own_blocks, incoming], axis=0)
    live_bool = jnp.arange(tile_values.shape[0], dtype=jnp.int32) < tile_count[0]
    live_mask = live_bool.astype(jnp.bfloat16)
    masked_tiles = tile_values * live_mask[:, None, None]
    picked = sources[tile_cols]
    products = jnp.einsum("tij,tjf->tif", masked_tiles, picked, preferred_element_type=jnp.float32)
    partial_value = jax.ops.segment_sum(products, tile_rows, num_segments=all_blocks)
    summed = lax.psum_scatter(partial_value, "col", scatter_dimension=0, tiled=True)
    hidden = summed.astype(jnp.bfloat16).reshape(half_blocks * block_size, width_in)
    output_rows = jnp.dot(hidden, weight, preferred_element_type=jnp.float32).astype(jnp.bfloat16)
    own_grad = lax.dot_general(
        cotangent, weight, (((1,), (1,)), ((), ())), preferred_element_type=jnp.float32
    ).astype(jnp.bfloat16)
    own_grad = own_grad.reshape(half_blocks, block_size, width_in)
    grad_blocks = lax.all_gather(own_grad, "col", axis=0, tiled=True)
    chosen = grad_blocks[tile_rows]
    back_terms = jnp.einsum(
        "tji,tjf->tif", masked_tiles, chosen, preferred_element_type=jnp.float32
    )
    spread = jax.ops.segment_sum(back_terms, tile_cols, num_segments=half_blocks + peer_count)
    returned = lax.all_to_all(spread[half_blocks:], "dom", split_axis=0, concat_axis=0, tiled=True)
    grad_total = spread[:half_blocks] + jax.ops.segment_sum(
        returned, send_blocks[0], num_segments=half_blocks
    )
    feature_grad = grad_total.astype(jnp.bfloat16).reshape(half_blocks * block_size, width_in)
    local_weight = lax.dot_general(
        hidden, cotangent, (((0,), (0,)), ((), ())), preferred_element_type=jnp.float32
    )
    local_weight = local_weight * jnp.float32(1.0 / node_total**0.5)
    col_share = lax.psum_scatter(local_weight, "col", scatter_dimension=0, tiled=True)
    dom_share = lax.psum(col_share, "dom")
    weight_grad = lax.all_gather(dom_share, "col", axis=0, tiled=True)
    return (output_rows, feature_grad, weight_grad)


def solution(mesh):
    return jax.shard_map(
        local,
        mesh=mesh,
        in_specs=(
            P(("dom", "col"), None),
            P(),
            P(("dom", "col"), None),
            P(("dom", "col"), None, None),
            P(("dom", "col")),
            P(("dom", "col")),
            P(("dom", "col")),
            P(("dom", "col"), None),
        ),
        out_specs=(P(("dom", "col"), None), P(("dom", "col"), None), P()),
        check_vma=False,
    )
```

profile of v0, /device:TPU:0, one launch (start us, length us, event | category | flops | bytes accessed | tf_op | source)
XLA Modules:
  0.0 214.5 jit_solution(6143368337666922137)
XLA Ops:
  7.2 0.0 copy-start
  7.2 0.0 copy-start.7
  7.2 0.0 copy-start.5
  7.2 0.7 fusion.6
  7.9 2.6 %gather_fusion = bf16[16,128,256]{2,1,0:T(8,128)(2,1)} fusion(bf16[4,128,256]{2,1,0:T(8,128)(2,1)} %bitcast.19, s32[1024]{0:T(1024)S(1)} %pad_clamp_fusion.2), kind=kCustom, calls=%fused_computation | custom fusion | bytes 2097216 | tf_op jit(solution)/shard_map/gather | solution.py:15
  10.5 8.4 %all-to-all-start = ((bf16[16,128,256]{2,1,0:T(8,128)(2,1)}), bf16[16,128,256]{2,1,0:T(8,128)(2,1)}, u32[]{:S(2)}, u32[]{:S(2)}) async-start(bf16[16,128,256]{2,1,0:T(8,128)(2,1)} %gather_fusion), calls=%async_computation | async-start | bytes 2097152 | tf_op jit(solution)/shard_map/all_to_all | solution.py:16
  19.5 0.0 copy-done.7
  19.6 0.0 copy-done
  19.6 0.0 copy-done.5
  19.6 0.3 convolution_convert_fusion
  19.9 2.2 %all_gather.6 = bf16[8,128,256]{2,1,0:T(8,128)(2,1)S(1)} all-gather(bf16[4,128,256]{2,1,0:T(8,128)(2,1)S(1)} %bitcast.23), channel_id=1, replica_groups=mesh['dom'=16,'col'=2] {'col'}, dimensions={0}, use_global_device_ids=true | all-gather | bytes 786432 | tf_op jit(solution)/shard_map/all_gather | solution.py:31
  22.0 0.7 gather_fusion.2
  22.8 4.9 %fusion = f32[40,128,256]{2,1,0:T(8,128)} fusion(bf16[40,128,256]{2,1,0:T(8,128)(2,1)S(1)} %gather_fusion.2, bf16[40,128,128]{2,1,0:T(8,128)(2,1)} %param.11, bf16[40]{0:T(256)(128)(2,1)S(1)} %compare_convert_fusion), kind=kOutput, calls=%fused_computation.10 | convolution fusion | flops 336199680 | bytes 9175120 | tf_op jit(solution)/shard_map/tji,tjf->tif/dot_general | solution.py:33
  27.7 0.0 copy-start.6
  27.7 0.3 broadcast_in_dim.24
  28.0 0.4 copy-done.6
  28.4 9.1 %scatter_fusion.1 = f32[20,128,256]{2,1,0:T(8,128)S(1)} fusion(f32[20,128,256]{2,1,0:T(8,128)S(1)} %broadcast_in_dim.24, s32[40]{0:T(128)S(1)} %copy-done.6, f32[40,128,256]{2,1,0:T(8,128)} %fusion), kind=kCustom, calls=%fused_computation.4 | custom fusion | flops 1310720 | bytes 15728800 | tf_op jit(solution)/shard_map/scatter-add | solution.py:36
  37.4 0.0 copy-start.2
  37.4 1.8 slice.15
  39.2 0.0 copy-start.3
  39.2 4.1 %all-to-all-done = bf16[16,128,256]{2,1,0:T(8,128)(2,1)} async-done(((bf16[16,128,256]{2,1,0:T(8,128)(2,1)}), bf16[16,128,256]{2,1,0:T(8,128)(2,1)}, u32[]{:S(2)}, u32[]{:S(2)}) %all-to-all-start) | async-done | bytes 1048608 | tf_op jit(solution)/shard_map/all_to_all | solution.py:16
  43.3 0.0 copy-done.2
  43.3 5.9 %all-to-all-start.1 = ((f32[16,128,256]{2,1,0:T(8,128)}), f32[16,128,256]{2,1,0:T(8,128)}, u32[]{:S(2)}, u32[]{:S(2)}) async-start(f32[16,128,256]{2,1,0:T(8,128)} %slice.15), calls=%async_computation.2 | async-start | bytes 4194304 | tf_op jit(solution)/shard_map/all_to_all | solution.py:37
  49.3 0.0 reduce-scatter.3.cloned.1.call-start
  49.3 0.0 copy-done.3
  49.4 1.3 pad_maximum_fusion
  50.7 0.0 copy-start.4
  50.7 2.4 %gather_fusion.1 = bf16[40,128,256]{2,1,0:T(8,128)(2,1)} fusion(bf16[20,128,256]{2,1,0:T(8,128)(2,1)S(1)} %pad_maximum_fusion, s32[1024]{0:T(1024)S(1)} %pad_clamp_fusion.1), kind=kCustom, calls=%fused_computation.1 | custom fusion | bytes 5243040 | tf_op jit(solution)/shard_map/gather | solution.py:21
  53.1 0.0 copy-done.4
  53.1 4.9 %fusion.2 = f32[40,128,256]{2,1,0:T(8,128)} fusion(bf16[40,128,256]{2,1,0:T(8,128)(2,1)} %gather_fusion.1, bf16[40,128,128]{2,1,0:T(8,128)(2,1)S(1)} %copy-done.4, bf16[40]{0:T(256)(128)(2,1)S(1)} %compare_convert_fusion), kind=kOutput, calls=%fused_computation.12 | convolution fusion | flops 336199680 | bytes 9175120 | tf_op jit(solution)/shard_map/tij,tjf->tif/dot_general | solution.py:22
  58.1 0.1 broadcast_in_dim.21
  58.1 9.0 %scatter_fusion = f32[8,128,256]{2,1,0:T(8,128)S(1)} fusion(f32[8,128,256]{2,1,0:T(8,128)S(1)} %broadcast_in_dim.21, s32[40]{0:T(128)S(1)} %copy-done.7, f32[40,128,256]{2,1,0:T(8,128)} %fusion.2), kind=kCustom, calls=%fused_computation.3 | custom fusion | flops 1310720 | bytes 15728800 | tf_op jit(solution)/shard_map/scatter-add | solution.py:23
  67.2 0.0 copy-start.1
  67.2 0.0 copy-start.8
  67.2 1.1 copy-done.1
  68.3 0.0 reduce-scatter.3.cloned.1.call-update
  68.3 0.0 reduce-scatter.5.cloned.1.call-start
  68.4 9.7 %reduce-scatter.3.cloned.1.call-done = f32[4,128,256]{2,1,0:T(8,128)} async-done(((f32[8,128,256]{2,1,0:T(8,128)}), f32[4,128,256]{2,1,0:T(8,128)}) %reduce-scatter.3.cloned.1.call-update) | async-done | bytes 524304 | tf_op jit(solution)/shard_map/reduce_scatter | solution.py:24
  78.1 1.1 convert_element_type.20
  79.1 1.0 convolution_multiply_fusion
  80.1 0.0 reduce-scatter.5.cloned.1.call-update
  80.1 0.0 all-reduce.2.cloned.1.call-start
  80.2 1.1 slice.14
  81.3 10.0 %all-to-all-done.1 = f32[16,128,256]{2,1,0:T(8,128)} async-done(((f32[16,128,256]{2,1,0:T(8,128)}), f32[16,128,256]{2,1,0:T(8,128)}, u32[]{:S(2)}, u32[]{:S(2)}) %all-to-all-start.1) | async-done | bytes 2097184 | tf_op jit(solution)/shard_map/all_to_all | solution.py:37
  91.2 0.0 copy-done.8
  91.2 3.5 %scatter_fusion.2 = f32[4,128,256]{2,1,0:T(8,128)S(1)} fusion(f32[4,128,256]{2,1,0:T(8,128)S(1)} %slice.14, s32[16]{0:T(128)S(1)} %bitcast.25, f32[16,128,256]{2,1,0:T(8,128)} %all-to-all-done.1), kind=kCustom, calls=%fused_computation.5 | custom fusion | flops 524288 | bytes 6291520 | tf_op jit(solution)/shard_map/scatter-add | solution.py:38
  94.7 0.7 convert_element_type.23
  95.4 0.0 reduce-scatter.5.cloned.1.call-done
  95.4 0.0 all-reduce.2.cloned.1.call-update
  95.5 0.9 convolution_convert_fusion.1
  96.4 108.7 %all-reduce.2.cloned.1.call-done = f32[128,256]{1,0:T(8,128)} async-done(((f32[128,256]{1,0:T(8,128)}), f32[128,256]{1,0:T(8,128)}) %all-reduce.2.cloned.1.call-update) | async-done | bytes 131088 | tf_op jit(solution)/shard_map/psum | solution.py:47
  205.1 2.2 %all_gather.7 = f32[256,256]{1,0:T(8,128)S(1)} all-gather(f32[128,256]{1,0:T(8,128)} %all-reduce.2.cloned.1.call-done), channel_id=1, replica_groups=mesh['dom'=16,'col'=2] {'col'}, dimensions={0}, use_global_device_ids=true | all-gather | bytes 393216 | tf_op jit(solution)/shard_map/all_gather | solution.py:48
  207.3 0.7 copy.20
  (6 shorter events, 0.0 us)
Async XLA Ops:
  7.2 12.4 %copy-start = (bf16[512,256]{1,0:T(8,128)(2,1)S(1)}, bf16[512,256]{1,0:T(8,128)(2,1)}, u32[]{:S(2)}) copy-start(bf16[512,256]{1,0:T(8,128)(2,1)} %param.10) | copy-start | bytes 786436
  7.2 12.4 %copy-start.7 = (s32[40]{0:T(128)S(1)}, s32[40]{0:T(128)}, u32[]{:S(2)}) copy-start(s32[40]{0:T(128)} %param.12) | copy-start | bytes 484
  7.2 12.4 %copy-start.5 = (bf16[256,256]{1,0:T(8,128)(2,1)S(1)}, bf16[256,256]{1,0:T(8,128)(2,1)}, u32[]{:S(2)}) copy-start(bf16[256,256]{1,0:T(8,128)(2,1)} %param.9) | copy-start | bytes 393220
  10.5 32.8 %all-to-all-start = ((bf16[16,128,256]{2,1,0:T(8,128)(2,1)}), bf16[16,128,256]{2,1,0:T(8,128)(2,1)}, u32[]{:S(2)}, u32[]{:S(2)}) async-start(bf16[16,128,256]{2,1,0:T(8,128)(2,1)} %gather_fusion), calls=%async_computation | async-start | bytes 2097152 | tf_op jit(solution)/shard_map/all_to_all | solution.py:16
  27.7 0.7 copy-start.6
  37.4 5.9 %copy-start.2 = (f32[20,128,256]{2,1,0:T(8,128)}, f32[20,128,256]{2,1,0:T(8,128)S(1)}, u32[]{:S(2)}) copy-start(f32[20,128,256]{2,1,0:T(8,128)S(1)} %scatter_fusion.1) | copy-start | bytes 7864324
  39.2 10.1 %copy-start.3 = (bf16[512,256]{1,0:T(8,128)(2,1)S(1)}, bf16[512,256]{1,0:T(8,128)(2,1)}, u32[]{:S(2)}) copy-start(bf16[512,256]{1,0:T(8,128)(2,1)} %param.8) | copy-start | bytes 786436
  43.3 47.9 %all-to-all-start.1 = ((f32[16,128,256]{2,1,0:T(8,128)}), f32[16,128,256]{2,1,0:T(8,128)}, u32[]{:S(2)}, u32[]{:S(2)}) async-start(f32[16,128,256]{2,1,0:T(8,128)} %slice.15), calls=%async_computation.2 | async-start | bytes 4194304 | tf_op jit(solution)/shard_map/all_to_all | solution.py:37
  49.3 28.8 %reduce-scatter.3.cloned.1.call-start = ((), (), s32[]{:S(2)}) async-start(), calls=%async_computation.4 | async-start | bytes 1572864 | tf_op jit(solution)/shard_map/reduce_scatter | solution.py:24
  50.7 2.4 %copy-start.4 = (bf16[40,128,128]{2,1,0:T(8,128)(2,1)S(1)}, bf16[40,128,128]{2,1,0:T(8,128)(2,1)}, u32[]{:S(2)}) copy-start(bf16[40,128,128]{2,1,0:T(8,128)(2,1)} %param.11) | copy-start | bytes 3932164
  67.2 1.1 copy-start.1
  67.2 24.0 %copy-start.8 = (s32[1,16]{1,0:T(1,128)S(1)}, s32[1,16]{1,0:T(1,128)}, u32[]{:S(2)}) copy-start(s32[1,16]{1,0:T(1,128)} %param.15) | copy-start | bytes 196
  68.3 27.1 %reduce-scatter.5.cloned.1.call-start = ((), (), s32[]{:S(2)}) async-start(), calls=%async_computation.5 | async-start | bytes 393216 | tf_op jit(solution)/shard_map/reduce_scatter | solution.py:46
  80.1 125.0 %all-reduce.2.cloned.1.call-start = ((), (), s32[]{:S(2)}) async-start(), calls=%async_computation.6 | async-start | bytes 262144 | tf_op jit(solution)/shard_map/psum | solution.py:47
Sparse Core Ops, SparseCore 0:
  68.4 9.5 reduce-scatter.2
  80.9 8.9 reduce-scatter.4
  95.6 109.4 all-reduce.1
where the time goes:
time: 215 us
  waiting for transfers between devices  133 us (62%)
  other arithmetic  25.5 us (12%)
  between operations  14.6 us (7%)
  starting transfers between devices  14.4 us (7%)
  matrix products  12 us (6%)
  local copies, waits for them, and re-layouts  11.1 us (5%)
  blocking collectives  4.37 us (2%)
    psum x1, waiting for transfers between devices, local(): dom_share = lax.psum(col_share, 'dom')  109 us
    all_to_all x1, waiting for transfers between devices, local(): lax.all_to_all(spread[half_blocks:], 'dom', split_axis=0, concat_axis=0,...  9.95 us
    reduce_scatter x1, waiting for transfers between devices, local(): lax.psum_scatter(partial_value, 'col', scatter_dimension=0, tiled=True)  9.71 us
    scatter-add x1, other arithmetic, local(): jax.ops.segment_sum(back_terms, tile_cols, num_segments=half_blocks + pee...  9.08 us
    scatter-add x1, other arithmetic, local(): jax.ops.segment_sum(products, tile_rows, num_segments=all_blocks)  9.04 us
    all_to_all x1, starting transfers between devices, local(): lax.all_to_all(outgoing, 'dom', split_axis=0, concat_axis=0, tiled=True)  8.39 us
    all_to_all x1, starting transfers between devices, local(): lax.all_to_all(spread[half_blocks:], 'dom', split_axis=0, concat_axis=0,...  5.93 us
    dot_general x1, matrix products, local(): jnp.einsum('tij,tjf->tif', masked_tiles, picked, preferred_element_type=j...  4.93 us
  transfers between devices with their start and end apart: 5, of which 4 were waited for; matrix products, arithmetic and copies ran while one was open for 20% of the time, Pallas kernels for 0%

commit v1 on v0

--- a/solution.py
+++ b/solution.py
@@ -34,7 +34,16 @@
         "tji,tjf->tif", masked_tiles, chosen, preferred_element_type=jnp.float32
     )
     spread = jax.ops.segment_sum(back_terms, tile_cols, num_segments=half_blocks + peer_count)
-    returned = lax.all_to_all(spread[half_blocks:], "dom", split_axis=0, concat_axis=0, tiled=True)
+    array = spread[half_blocks:]
+    ways, here = (lax.axis_size("dom"), lax.axis_index("dom"))
+    width = array.shape[0] // ways
+    turned = jnp.roll(array, -here * width, axis=0)
+    got = [lax.slice_in_dim(turned, 0, width, axis=0)]
+    for far in range(1, ways):
+        sent = lax.slice_in_dim(turned, far * width, (far + 1) * width, axis=0)
+        got.append(lax.ppermute(sent, "dom", [(d, (d + far) % ways) for d in range(ways)]))
+    line = jnp.concatenate(got[::-1], axis=0)
+    returned = jnp.roll(line, (here + 1) * got[0].shape[0], axis=0)
     grad_total = spread[:half_blocks] + jax.ops.segment_sum(
         returned, send_blocks[0], num_segments=half_blocks
     )

time: 215 us -> 271 us (1.26)
  starting transfers between devices: 14.4 us -> 50.8 us
  local copies, waits for them, and re-layouts: 11.1 us -> 29.7 us
    ppermute x0 -> x15, starting transfers between devices: none -> 42.3 us  [local(): lax.ppermute(sent, 'dom', [(d, (d + far) % ways) for d in range(ways)])]
    unnamed x19 -> x38, local copies, waits for them, and re-layouts: 2.2 us -> 17.5 us
    all_to_all x1, waiting for transfers between devices: 4.13 us -> 18.8 us  [local(): lax.all_to_all(outgoing, 'dom', split_axis=0, concat_axis=0, tiled=True)]
    all_to_all x1 -> x0, waiting for transfers between devices: 9.95 us -> none  [local(): lax.all_to_all(spread[half_blocks:], 'dom', split_axis=0, concat_axis=0,...]
    reduce_scatter x1, waiting for transfers between devices: 9.71 us -> 0.01 us  [local(): lax.psum_scatter(partial_value, 'col', scatter_dimension=0, tiled=True)]
    all_to_all x1 -> x0, starting transfers between devices: 5.93 us -> none  [local(): lax.all_to_all(spread[half_blocks:], 'dom', split_axis=0, concat_axis=0,...]
    ppermute x0 -> x15, waiting for transfers between devices: none -> 5.62 us  [local(): lax.ppermute(sent, 'dom', [(d, (d + far) % ways) for d in range(ways)])]
    concatenate x0 -> x2, other arithmetic: none -> 4.07 us  [the longest x1 2.04 us: local(): turned = jnp.roll(array, -here * width, axis=0)]
  transfers between devices with their start and end apart: 5 -> 19, of which waited for: 4 -> 5; matrix products, arithmetic and copies ran while one was open for 20% -> 17% of each run, Pallas kernels for 0% -> 0%
where the time goes in v1:
time: 271 us; the launch traced here: 270 us
  waiting for transfers between devices  131 us (48%)
  starting transfers between devices  50.8 us (19%)
  local copies, waits for them, and re-layouts  29.7 us (11%)
  other arithmetic  27 us (10%)
  between operations  14.6 us (5%)
  matrix products  12.5 us (5%)
  blocking collectives  4.37 us (2%)
    psum x1, waiting for transfers between devices, local(): dom_share = lax.psum(col_share, 'dom')  107 us
    ppermute x15, starting transfers between devices, local(): lax.ppermute(sent, 'dom', [(d, (d + far) % ways) for d in range(ways)])  42.3 us
    all_to_all x1, waiting for transfers between devices, local(): lax.all_to_all(outgoing, 'dom', split_axis=0, concat_axis=0, tiled=True)  18.8 us
    unnamed x38, local copies, waits for them, and re-layouts  17.5 us
    scatter-add x1, other arithmetic, local(): jax.ops.segment_sum(back_terms, tile_cols, num_segments=half_blocks + pee...  9.09 us
    scatter-add x1, other arithmetic, local(): jax.ops.segment_sum(products, tile_rows, num_segments=all_blocks)  9.04 us
    all_to_all x1, starting transfers between devices, local(): lax.all_to_all(outgoing, 'dom', split_axis=0, concat_axis=0, tiled=True)  8.34 us
    ppermute x15, waiting for transfers between devices, local(): lax.ppermute(sent, 'dom', [(d, (d + far) % ways) for d in range(ways)])  5.62 us
  transfers between devices with their start and end apart: 19, of which 5 were waited for; matrix products, arithmetic and copies ran while one was open for 17% of the time, Pallas kernels for 0%

profile of v1, /device:TPU:0, one launch (start us, length us, event | category | flops | bytes accessed | tf_op | source)
XLA Modules:
  0.0 270.3 jit_solution(14947112726077964496)
XLA Ops:
  7.2 0.7 fusion.8
  7.9 2.6 gather_fusion
  10.5 8.3 %all-to-all-start = ((bf16[16,128,256]{2,1,0:T(8,128)(2,1)}), bf16[16,128,256]{2,1,0:T(8,128)(2,1)S(1)}, u32[]{:S(2)}, u32[]{:S(2)}) async-start(bf16[16,128,256]{2,1,0:T(8,128)(2,1)} %gather_fusion), calls=%async_computation | async-start | bytes 2097152 | tf_op jit(solution)/shard_map/all_to_all | solution.py:16
  18.8 0.0 reduce-scatter.3.cloned.1.call-start
  19.6 0.3 convolution_convert_fusion
  19.9 2.2 all_gather.6
  22.0 2.3 gather_fusion.2
  24.4 18.8 %all-to-all-done = bf16[16,128,256]{2,1,0:T(8,128)(2,1)S(1)} async-done(((bf16[16,128,256]{2,1,0:T(8,128)(2,1)}), bf16[16,128,256]{2,1,0:T(8,128)(2,1)S(1)}, u32[]{:S(2)}, u32[]{:S(2)}) %all-to-all-start) | async-done | bytes 1048608 | tf_op jit(solution)/shard_map/all_to_all | solution.py:16
  43.2 0.1 pad_maximum_fusion
  43.4 2.4 gather_fusion.1
  45.8 5.0 %fusion.4 = f32[40,128,256]{2,1,0:T(8,128)} fusion(bf16[40,128,256]{2,1,0:T(8,128)(2,1)} %gather_fusion.1, bf16[40,128,128]{2,1,0:T(8,128)(2,1)S(1)} %copy-done.4, bf16[40]{0:T(256)(128)(2,1)S(1)} %compare_convert_fusion), kind=kOutput, calls=%fused_computation.18 | convolution fusion | flops 336199680 | bytes 9175120 | tf_op jit(solution)/shard_map/tij,tjf->tif/dot_general | solution.py:22
  50.8 0.1 broadcast_in_dim.21
  50.9 9.0 %scatter_fusion = f32[8,128,256]{2,1,0:T(8,128)S(1)} fusion(f32[8,128,256]{2,1,0:T(8,128)S(1)} %broadcast_in_dim.21, s32[40]{0:T(128)S(1)} %copy-done.8, f32[40,128,256]{2,1,0:T(8,128)} %fusion.4), kind=kCustom, calls=%fused_computation.3 | custom fusion | flops 1310720 | bytes 15728800 | tf_op jit(solution)/shard_map/scatter-add | solution.py:23
  59.9 1.0 copy-done.1
  61.0 5.4 %fusion.2 = f32[40,128,256]{2,1,0:T(8,128)} fusion(bf16[40,128,256]{2,1,0:T(8,128)(2,1)} %gather_fusion.2, bf16[40,128,128]{2,1,0:T(8,128)(2,1)S(1)} %copy-done.4, bf16[40]{0:T(256)(128)(2,1)S(1)} %compare_convert_fusion), kind=kOutput, calls=%fused_computation.16 | convolution fusion | flops 336199680 | bytes 9175120 | tf_op jit(solution)/shard_map/tji,tjf->tif/dot_general | solution.py:33
  66.4 0.3 broadcast_in_dim.24
  66.7 9.1 %scatter_fusion.1 = f32[20,128,256]{2,1,0:T(8,128)S(1)} fusion(f32[20,128,256]{2,1,0:T(8,128)S(1)} %broadcast_in_dim.24, s32[40]{0:T(128)S(1)} %copy-done.9, f32[40,128,256]{2,1,0:T(8,128)} %fusion.2), kind=kCustom, calls=%fused_computation.4 | custom fusion | flops 1310720 | bytes 15728800 | tf_op jit(solution)/shard_map/scatter-add | solution.py:36
  75.8 1.6 slice.79
  77.3 2.0 fusion.1
  79.4 1.3 copy-done.2
  80.7 1.3 fusion.9
  82.0 4.8 %collective-permute-start = (f32[1,128,256]{2,1,0:T(8,128)}, f32[1,128,256]{2,1,0:T(8,128)}, u32[]{:S(2)}, u32[]{:S(2)}) collective-permute-start(f32[1,128,256]{2,1,0:T(8,128)} %get-tuple-element.18), channel_id=1, source_target_pairs={{0,30},{2,0},{4,2},{6,4},{8,6},{10,8},{12,10},{14,12},{16,14},{18,... | collective-permute-start | bytes 393224 | tf_op jit(solution)/shard_map/ppermute | solution.py:44
  86.8 0.3 collective-permute-start.2
  87.1 3.0 %collective-permute-start.3 = (f32[1,128,256]{2,1,0:T(8,128)}, f32[1,128,256]{2,1,0:T(8,128)}, u32[]{:S(2)}, u32[]{:S(2)}) collective-permute-start(f32[1,128,256]{2,1,0:T(8,128)} %get-tuple-element.15), channel_id=1, source_target_pairs={{0,24},{2,26},{4,28},{6,30},{8,0},{10,2},{12,4},{14,6},{16,8},{18,... | collective-permute-start | bytes 393224 | tf_op jit(solution)/shard_map/ppermute | solution.py:44
  90.1 0.1 collective-permute-start.4
  90.3 0.7 collective-permute-done
  91.0 2.6 collective-permute-start.5
  93.7 1.6 constant_dynamic-update-slice_fusion.14
  95.2 1.1 collective-permute-start.6
  96.4 1.6 constant_dynamic-update-slice_fusion.13
  98.0 1.7 collective-permute-start.7
  99.6 1.6 constant_dynamic-update-slice_fusion.12
  101.2 2.2 collective-permute-start.8
  103.4 1.6 constant_dynamic-update-slice_fusion.11
  105.0 4.1 %collective-permute-start.9 = (f32[1,128,256]{2,1,0:T(8,128)}, f32[1,128,256]{2,1,0:T(8,128)S(1)}, u32[]{:S(2)}, u32[]{:S(2)}) collective-permute-start(f32[1,128,256]{2,1,0:T(8,128)} %get-tuple-element.9), channel_id=1, source_target_pairs={{0,12},{2,14},{4,16},{6,18},{8,20},{10,22},{12,24},{14,26},{16,28}... | collective-permute-start | bytes 393224 | tf_op jit(solution)/shard_map/ppermute | solution.py:44
  109.1 1.6 constant_dynamic-update-slice_fusion.10
  110.7 1.7 collective-permute-start.10
  112.3 0.7 constant_dynamic-update-slice_fusion.9
  113.0 11.3 %collective-permute-start.11 = (f32[1,128,256]{2,1,0:T(8,128)}, f32[1,128,256]{2,1,0:T(8,128)S(1)}, u32[]{:S(2)}, u32[]{:S(2)}) collective-permute-start(f32[1,128,256]{2,1,0:T(8,128)} %get-tuple-element.7), channel_id=1, source_target_pairs={{0,8},{2,10},{4,12},{6,14},{8,16},{10,18},{12,20},{14,22},{16,24},... | collective-permute-start | bytes 393224 | tf_op jit(solution)/shard_map/ppermute | solution.py:44
  124.3 0.7 constant_dynamic-update-slice_fusion.8
  124.9 4.2 %collective-permute-done.7 = f32[1,128,256]{2,1,0:T(8,128)S(1)} collective-permute-done((f32[1,128,256]{2,1,0:T(8,128)}, f32[1,128,256]{2,1,0:T(8,128)S(1)}, u32[]{:S(2)}, u32[]{:S(2)}) %collective-permute-start.7) | collective-permute-done | bytes 131104 | tf_op jit(solution)/shard_map/ppermute | solution.py:44
  129.1 1.1 collective-permute-start.12
  130.2 0.7 constant_dynamic-update-slice_fusion.7
  130.9 1.5 collective-permute-start.13
  132.3 0.7 constant_dynamic-update-slice_fusion.6
  133.0 6.7 %collective-permute-start.14 = (f32[1,128,256]{2,1,0:T(8,128)S(1)}, f32[1,128,256]{2,1,0:T(8,128)S(1)}, u32[]{:S(2)}, u32[]{:S(2)}) collective-permute-start(f32[1,128,256]{2,1,0:T(8,128)S(1)} %copy-done.6), channel_id=1, source_target_pairs={{0,2},{2,4},{4,6},{6,8},{8,10},{10,12},{12,14},{14,16},{16,18},{18... | collective-permute-start | bytes 393224 | tf_op jit(solution)/shard_map/ppermute | solution.py:44
  139.7 0.7 constant_dynamic-update-slice_fusion.5
  140.4 0.7 collective-permute-done.10
  141.1 0.7 constant_dynamic-update-slice_fusion.4
  141.7 0.7 constant_dynamic-update-slice_fusion.3
  142.4 0.7 constant_dynamic-update-slice_fusion.2
  143.1 1.1 convert_element_type.20
  144.2 1.0 convolution_multiply_fusion
  145.2 0.0 all-reduce.2.cloned.1.call-start
  145.2 0.7 constant_dynamic-update-slice_fusion.1
  145.9 0.7 constant_dynamic-update-slice_fusion
  146.5 1.6 slice_dynamic-update-slice_fusion
  148.1 2.0 fusion
  150.2 2.2 scatter_fusion.2
  152.3 0.7 convert_element_type.23
  153.1 0.9 convolution_convert_fusion.1
  154.0 106.9 %all-reduce.2.cloned.1.call-done = f32[128,256]{1,0:T(8,128)} async-done(((f32[128,256]{1,0:T(8,128)}), f32[128,256]{1,0:T(8,128)}) %all-reduce.2.cloned.1.call-update) | async-done | bytes 131088 | tf_op jit(solution)/shard_map/psum | solution.py:56
  260.9 2.2 all_gather.7
  263.1 0.7 copy.35
  (46 shorter events, 0.2 us)
Async XLA Ops:
  7.2 12.4 %copy-start = (bf16[512,256]{1,0:T(8,128)(2,1)S(1)}, bf16[512,256]{1,0:T(8,128)(2,1)}, u32[]{:S(2)}) copy-start(bf16[512,256]{1,0:T(8,128)(2,1)} %param.12) | copy-start | bytes 786436
  7.9 11.7 %copy-start.8 = (s32[40]{0:T(128)S(1)}, s32[40]{0:T(128)}, u32[]{:S(2)}) copy-start(s32[40]{0:T(128)} %param.14) | copy-start | bytes 484
  7.9 11.7 %copy-start.5 = (bf16[256,256]{1,0:T(8,128)(2,1)S(1)}, bf16[256,256]{1,0:T(8,128)(2,1)}, u32[]{:S(2)}) copy-start(bf16[256,256]{1,0:T(8,128)(2,1)} %param.11) | copy-start | bytes 393220
  10.5 32.7 %all-to-all-start = ((bf16[16,128,256]{2,1,0:T(8,128)(2,1)}), bf16[16,128,256]{2,1,0:T(8,128)(2,1)S(1)}, u32[]{:S(2)}, u32[]{:S(2)}) async-start(bf16[16,128,256]{2,1,0:T(8,128)(2,1)} %gather_fusion), calls=%async_computation | async-start | bytes 2097152 | tf_op jit(solution)/shard_map/all_to_all | solution.py:16
  18.8 124.2 %reduce-scatter.3.cloned.1.call-start = ((), (), s32[]{:S(2)}) async-start(), calls=%async_computation.3 | async-start | bytes 1572864 | tf_op jit(solution)/shard_map/reduce_scatter | solution.py:24
  22.0 2.3 copy-start.9
  22.0 21.2 %copy-start.3 = (bf16[512,256]{1,0:T(8,128)(2,1)S(1)}, bf16[512,256]{1,0:T(8,128)(2,1)}, u32[]{:S(2)}) copy-start(bf16[512,256]{1,0:T(8,128)(2,1)} %param.10) | copy-start | bytes 786436
  43.4 2.5 copy-start.4
  59.9 1.0 copy-start.1
  61.0 92.1 %reduce-scatter.5.cloned.1.call-start = ((), (), s32[]{:S(2)}) async-start(), calls=%async_computation.4 | async-start | bytes 393216 | tf_op jit(solution)/shard_map/reduce_scatter | solution.py:55
  79.4 1.3 copy-start.2
  82.0 9.1 %collective-permute-start = (f32[1,128,256]{2,1,0:T(8,128)}, f32[1,128,256]{2,1,0:T(8,128)}, u32[]{:S(2)}, u32[]{:S(2)}) collective-permute-start(f32[1,128,256]{2,1,0:T(8,128)} %get-tuple-element.18), channel_id=1, source_target_pairs={{0,30},{2,0},{4,2},{6,4},{8,6},{10,8},{12,10},{14,12},{16,14},{18,... | collective-permute-start | bytes 393224 | tf_op jit(solution)/shard_map/ppermute | solution.py:44
  86.8 8.4 %collective-permute-start.1 = (f32[1,128,256]{2,1,0:T(8,128)}, f32[1,128,256]{2,1,0:T(8,128)}, u32[]{:S(2)}, u32[]{:S(2)}) collective-permute-start(f32[1,128,256]{2,1,0:T(8,128)} %get-tuple-element.17), channel_id=1, source_target_pairs={{0,28},{2,30},{4,0},{6,2},{8,4},{10,6},{12,8},{14,10},{16,12},{18,... | collective-permute-start | bytes 393224 | tf_op jit(solution)/shard_map/ppermute | solution.py:44
  86.8 11.2 %collective-permute-start.2 = (f32[1,128,256]{2,1,0:T(8,128)}, f32[1,128,256]{2,1,0:T(8,128)}, u32[]{:S(2)}, u32[]{:S(2)}) collective-permute-start(f32[1,128,256]{2,1,0:T(8,128)} %get-tuple-element.16), channel_id=1, source_target_pairs={{0,26},{2,28},{4,30},{6,0},{8,2},{10,4},{12,6},{14,8},{16,10},{18,... | collective-permute-start | bytes 393224 | tf_op jit(solution)/shard_map/ppermute | solution.py:44
  87.1 14.1 %collective-permute-start.3 = (f32[1,128,256]{2,1,0:T(8,128)}, f32[1,128,256]{2,1,0:T(8,128)}, u32[]{:S(2)}, u32[]{:S(2)}) collective-permute-start(f32[1,128,256]{2,1,0:T(8,128)} %get-tuple-element.15), channel_id=1, source_target_pairs={{0,24},{2,26},{4,28},{6,30},{8,0},{10,2},{12,4},{14,6},{16,8},{18,... | collective-permute-start | bytes 393224 | tf_op jit(solution)/shard_map/ppermute | solution.py:44
  90.1 14.9 %collective-permute-start.4 = (f32[1,128,256]{2,1,0:T(8,128)}, f32[1,128,256]{2,1,0:T(8,128)}, u32[]{:S(2)}, u32[]{:S(2)}) collective-permute-start(f32[1,128,256]{2,1,0:T(8,128)} %get-tuple-element.14), channel_id=1, source_target_pairs={{0,22},{2,24},{4,26},{6,28},{8,30},{10,0},{12,2},{14,4},{16,6},{18... | collective-permute-start | bytes 393224 | tf_op jit(solution)/shard_map/ppermute | solution.py:44
  90.3 40.6 %copy-start.7 = (f32[1,128,256]{2,1,0:T(8,128)S(1)}, f32[1,128,256]{2,1,0:T(8,128)}, u32[]{:S(2)}) copy-start(f32[1,128,256]{2,1,0:T(8,128)} %get-tuple-element.5) | copy-start | bytes 393220
  90.3 42.7 %copy-start.6 = (f32[1,128,256]{2,1,0:T(8,128)S(1)}, f32[1,128,256]{2,1,0:T(8,128)}, u32[]{:S(2)}) copy-start(f32[1,128,256]{2,1,0:T(8,128)} %get-tuple-element.4) | copy-start | bytes 393220
  91.0 19.6 %collective-permute-start.5 = (f32[1,128,256]{2,1,0:T(8,128)}, f32[1,128,256]{2,1,0:T(8,128)S(1)}, u32[]{:S(2)}, u32[]{:S(2)}) collective-permute-start(f32[1,128,256]{2,1,0:T(8,128)} %get-tuple-element.13), channel_id=1, source_target_pairs={{0,20},{2,22},{4,24},{6,26},{8,28},{10,30},{12,0},{14,2},{16,4},{1... | collective-permute-start | bytes 393224 | tf_op jit(solution)/shard_map/ppermute | solution.py:44
  95.2 17.8 %collective-permute-start.6 = (f32[1,128,256]{2,1,0:T(8,128)}, f32[1,128,256]{2,1,0:T(8,128)S(1)}, u32[]{:S(2)}, u32[]{:S(2)}) collective-permute-start(f32[1,128,256]{2,1,0:T(8,128)} %get-tuple-element.12), channel_id=1, source_target_pairs={{0,18},{2,20},{4,22},{6,24},{8,26},{10,28},{12,30},{14,0},{16,2},{... | collective-permute-start | bytes 393224 | tf_op jit(solution)/shard_map/ppermute | solution.py:44
  98.0 31.1 %collective-permute-start.7 = (f32[1,128,256]{2,1,0:T(8,128)}, f32[1,128,256]{2,1,0:T(8,128)S(1)}, u32[]{:S(2)}, u32[]{:S(2)}) collective-permute-start(f32[1,128,256]{2,1,0:T(8,128)} %get-tuple-element.11), channel_id=1, source_target_pairs={{0,16},{2,18},{4,20},{6,22},{8,24},{10,26},{12,28},{14,30},{16,0},... | collective-permute-start | bytes 393224 | tf_op jit(solution)/shard_map/ppermute | solution.py:44
  101.2 29.7 %collective-permute-start.8 = (f32[1,128,256]{2,1,0:T(8,128)}, f32[1,128,256]{2,1,0:T(8,128)S(1)}, u32[]{:S(2)}, u32[]{:S(2)}) collective-permute-start(f32[1,128,256]{2,1,0:T(8,128)} %get-tuple-element.10), channel_id=1, source_target_pairs={{0,14},{2,16},{4,18},{6,20},{8,22},{10,24},{12,26},{14,28},{16,30}... | collective-permute-start | bytes 393224 | tf_op jit(solution)/shard_map/ppermute | solution.py:44
  105.0 28.0 %collective-permute-start.9 = (f32[1,128,256]{2,1,0:T(8,128)}, f32[1,128,256]{2,1,0:T(8,128)S(1)}, u32[]{:S(2)}, u32[]{:S(2)}) collective-permute-start(f32[1,128,256]{2,1,0:T(8,128)} %get-tuple-element.9), channel_id=1, source_target_pairs={{0,12},{2,14},{4,16},{6,18},{8,20},{10,22},{12,24},{14,26},{16,28}... | collective-permute-start | bytes 393224 | tf_op jit(solution)/shard_map/ppermute | solution.py:44
  110.7 30.4 %collective-permute-start.10 = (f32[1,128,256]{2,1,0:T(8,128)}, f32[1,128,256]{2,1,0:T(8,128)S(1)}, u32[]{:S(2)}, u32[]{:S(2)}) collective-permute-start(f32[1,128,256]{2,1,0:T(8,128)} %get-tuple-element.8), channel_id=1, source_target_pairs={{0,10},{2,12},{4,14},{6,16},{8,18},{10,20},{12,22},{14,24},{16,26}... | collective-permute-start | bytes 393224 | tf_op jit(solution)/shard_map/ppermute | solution.py:44
  113.0 28.7 %collective-permute-start.11 = (f32[1,128,256]{2,1,0:T(8,128)}, f32[1,128,256]{2,1,0:T(8,128)S(1)}, u32[]{:S(2)}, u32[]{:S(2)}) collective-permute-start(f32[1,128,256]{2,1,0:T(8,128)} %get-tuple-element.7), channel_id=1, source_target_pairs={{0,8},{2,10},{4,12},{6,14},{8,16},{10,18},{12,20},{14,22},{16,24},... | collective-permute-start | bytes 393224 | tf_op jit(solution)/shard_map/ppermute | solution.py:44
  129.1 13.3 %collective-permute-start.12 = (f32[1,128,256]{2,1,0:T(8,128)}, f32[1,128,256]{2,1,0:T(8,128)S(1)}, u32[]{:S(2)}, u32[]{:S(2)}) collective-permute-start(f32[1,128,256]{2,1,0:T(8,128)} %get-tuple-element.6), channel_id=1, source_target_pairs={{0,6},{2,8},{4,10},{6,12},{8,14},{10,16},{12,18},{14,20},{16,22},{... | collective-permute-start | bytes 393224 | tf_op jit(solution)/shard_map/ppermute | solution.py:44
  130.9 14.3 %collective-permute-start.13 = (f32[1,128,256]{2,1,0:T(8,128)S(1)}, f32[1,128,256]{2,1,0:T(8,128)S(1)}, u32[]{:S(2)}, u32[]{:S(2)}) collective-permute-start(f32[1,128,256]{2,1,0:T(8,128)S(1)} %copy-done.7), channel_id=1, source_target_pairs={{0,4},{2,6},{4,8},{6,10},{8,12},{10,14},{12,16},{14,18},{16,20},{1... | collective-permute-start | bytes 393224 | tf_op jit(solution)/shard_map/ppermute | solution.py:44
  133.0 12.9 %collective-permute-start.14 = (f32[1,128,256]{2,1,0:T(8,128)S(1)}, f32[1,128,256]{2,1,0:T(8,128)S(1)}, u32[]{:S(2)}, u32[]{:S(2)}) collective-permute-start(f32[1,128,256]{2,1,0:T(8,128)S(1)} %copy-done.6), channel_id=1, source_target_pairs={{0,2},{2,4},{4,6},{6,8},{8,10},{10,12},{12,14},{14,16},{16,18},{18... | collective-permute-start | bytes 393224 | tf_op jit(solution)/shard_map/ppermute | solution.py:44
  145.2 115.7 %all-reduce.2.cloned.1.call-start = ((), (), s32[]{:S(2)}) async-start(), calls=%async_computation.5 | async-start | bytes 262144 | tf_op jit(solution)/shard_map/psum | solution.py:56
  148.1 2.0 copy-start.10
Sparse Core Ops, SparseCore 0:
  61.1 8.6 reduce-scatter.2
  145.3 3.5 reduce-scatter.4
  154.4 106.5 all-reduce.1
